TPU v7x, 32 devices: a whole 2x2x4 slice. The times are simulated.
32 devices in a mesh: region: 8 (over z, x), member: 4 (over y, core).
Axes of the slice: x: 2, y: 2, z: 4, core: 2. Of those that a mesh axis runs over, the one named last changes fastest.
Arguments:
- members: float32 [256, 128, 1024], P('member', 'region'), may hold values from -6 to 6
- obs_value: float32 [128, 1024], P('region'), may hold values from -6 to 6
- obs_precision: float32 [128, 1024], P('region'), may hold values from 0.02 to 200
- obs_index: int32 [128, 1024], P('region'), may hold values from 0 to 1023, as said below
- obs_count: int32 [128], P('region'), may hold values from 256 to 1024
Outputs:
- analysis: float32 [256, 128, 1024], P('member', 'region')
Inputs may be any that keep to these rules, and one draw needn't show every extreme that they name: `obs_count`: slots of a tile from its count onward are empty. `obs_index`: position within its own tile.
All inputs are finite; a program needn't handle non-finite values.
Results may differ from a plain program's by a relative error of at most 0.0005.
Values sent between devices are 32-bit elements; how exact they have to be, the bound alone decides.
A program may use at most 64 MiB of HBM per device.

v0:
```python
import functools
import math

import jax
import jax.numpy as jnp
from jax import lax
from jax.experimental import pallas as pl
from jax.experimental.pallas import tpu as pltpu
from jax.sharding import PartitionSpec as P

ITERS = 12
LANES = 128
F32 = jnp.float32
BF16 = jnp.bfloat16


def split3(x):
    a = x.astype(BF16)
    rest = x - a.astype(F32)
    b = rest.astype(BF16)
    return a, b, (rest - b.astype(F32)).astype(BF16)


def dot(a, b):
    return jnp.dot(a, b, preferred_element_type=F32)


def dot_nt(a, b):
    return lax.dot_general(a, b, (((1,), (1,)), ((), ())), preferred_element_type=F32)


def product(a, b):
    a1, a2, a3 = a
    b1, b2, b3 = b
    left = jnp.concatenate([a1, a3, a2, a1, a2, a1], axis=1)
    right = jnp.concatenate([b3, b1, b2, b2, b1, b1], axis=0)
    return dot(left, right)


def gram_kernel(x_ref, index_ref, value_ref, precision_ref, out_ref):
    states = x_ref[0]
    size, width = states.shape
    half = size // 2
    groups = width // LANES
    places, exact = index_ref[0], precision_ref[0]
    slots = places.shape[1]

    high = lax.shift_right_logical(places, 7)
    low = lax.bitwise_and(places, LANES - 1)
    rows = lax.broadcasted_iota(jnp.int32, (groups, slots), 0) == high
    both = jnp.concatenate(
        [jnp.where(rows, exact, 0.0), jnp.where(rows, exact * value_ref[0], 0.0)], axis=0
    )
    one_hot = jnp.where(
        lax.broadcasted_iota(jnp.int32, (LANES, slots), 0) == low, 1.0, 0.0
    ).astype(BF16)
    e1, e2, e3 = split3(both)
    sums = dot_nt(e3, one_hot) + dot_nt(e2, one_hot) + dot_nt(e1, one_hot)
    c = jnp.concatenate([sums[i : i + 1] for i in range(groups)], axis=1)
    d = jnp.concatenate([sums[groups + i : groups + i + 1] for i in range(groups)], axis=1)

    average = jnp.sum(states, axis=0, keepdims=True) / size
    deviation = states - average
    s1, s2, s3 = split3(deviation * jnp.sqrt(c))
    cross = dot_nt(s1, s3) + dot_nt(s1, s2)
    own = (dot_nt(s2, s2) + (cross + cross.T)) + dot_nt(s1, s1)

    pulled = deviation * (d - c * average)
    folded = pulled[:, :LANES]
    for i in range(1, groups):
        folded = folded + pulled[:, i * LANES : (i + 1) * LANES]
    right = jnp.sum(folded.T, axis=0, keepdims=True)

    row = lax.broadcasted_iota(jnp.int32, (half, half), 0)
    col = lax.broadcasted_iota(jnp.int32, (half, half), 1)
    first, last = own[:half, :half], own[half:, half:]
    diagonal = jnp.sum(jnp.where(row == col, last, 0.0), axis=0, keepdims=True)
    out_ref[0, :half, :half] = own[:half, half:]
    out_ref[0, :half, half:] = jnp.where(row <= col, first, last)
    tail = jnp.concatenate([right, jnp.concatenate([diagonal, diagonal], axis=1)], axis=0)
    out_ref[0, half:, :] = jnp.concatenate([tail, jnp.zeros((6, size), F32)], axis=0)


def analysis_kernel(own_ref, west_ref, east_ref, x_ref, out_ref, u_ref, z_ref):
    tiles, size, width = x_ref.shape
    half = size // 2
    row = lax.broadcasted_iota(jnp.int32, (size, size), 0)
    col = lax.broadcasted_iota(jnp.int32, (size, size), 1)
    identity = jnp.where(row == col, 1.0, 0.0).astype(F32)
    small_row, small_col = row[:half, :half], col[:half, :half]
    rights, scales = [], []

    def growth(u, z):
        x = split3(u if z is None else product(z, u))
        plain = u if z is None else x[0].astype(F32) + x[1].astype(F32) + x[2].astype(F32)
        squared = product(x, x)
        inner = (1 / 16) * squared - (9 / 16) * plain
        outer = product(split3(squared), split3(inner))
        return (36 / 16) * identity - (39 / 16) * plain + (27 / 16) * squared + outer

    for t in range(tiles):
        packed = own_ref[t] + 0.5 * (west_ref[t] + east_ref[t])
        upper, mixed = packed[:half, :half], packed[:half, half:]
        rights.append(packed[half : half + 1])
        diagonal = packed[half + 1 : half + 2, :half]
        turned = mixed.T
        first = jnp.where(small_row <= small_col, mixed, turned)
        last = jnp.where(small_row > small_col, mixed, turned)
        last = jnp.where(small_row == small_col, diagonal, last)
        gram = jnp.concatenate(
            [
                jnp.concatenate([first, upper], axis=1),
                jnp.concatenate([upper.T, last], axis=1),
            ],
            axis=0,
        )
        system = (size - 1.0) * identity + gram
        total = jnp.sum(jnp.sum(system * system, axis=0, keepdims=True), axis=1, keepdims=True)
        scale = jnp.sqrt(total + 1e-6)
        scales.append(scale)
        u = system / scale
        g = growth(u, None)
        z_ref[t] = g
        u_ref[t] = product(split3(u), split3(g))

    def two_steps(_, carry):
        for t in range(tiles):
            u, z = split3(u_ref[t]), split3(z_ref[t])
            g = split3(growth(u, z))
            u_ref[t] = product(u, g)
            z_ref[t] = product(g, z)
        return carry

    lax.fori_loop(0, ITERS // 2 - 2, two_steps, 0)

    for t in range(tiles):
        u, z = split3(u_ref[t]), split3(z_ref[t])
        inverse = product(split3(growth(u, z)), z) / jnp.sqrt(scales[t])
        pulled = jnp.sum(inverse * rights[t], axis=1, keepdims=True)
        shift = jnp.sum(inverse * pulled, axis=0, keepdims=True)
        weights = math.sqrt(size - 1.0) * inverse + shift
        average = jnp.sum(x_ref[t], axis=0, keepdims=True) / size
        w1, w2, _ = split3(weights)
        d1, d2, _ = split3(x_ref[t] - average)
        left = jnp.concatenate([w2, w1, w1], axis=1)
        right = jnp.concatenate([d1, d2, d1], axis=0)
        out_ref[t] = average + dot(left, right)


def block(*shape):
    return pl.BlockSpec(shape, lambda i: (i,) + (0,) * (len(shape) - 1))


def grams(states, places, observed, accuracy):
    owned, size, width = states.shape
    slots = places.shape[1]
    table = block(1, 1, slots)
    return pl.pallas_call(
        gram_kernel,
        grid=(owned,),
        in_specs=[block(1, size, width), table, table, table],
        out_specs=block(1, size // 2 + 8, size),
        out_shape=jax.ShapeDtypeStruct((owned, size // 2 + 8, size), F32),
        cost_estimate=pl.CostEstimate(
            flops=owned * 12 * size * size * width, bytes_accessed=states.size * 4, transcendentals=0
        ),
    )(states, places[:, None], observed[:, None], accuracy[:, None])


def analyses(own, west, east, states):
    owned, size, width = states.shape
    tiles = 2 if owned % 2 == 0 else 1
    packed = block(tiles, size // 2 + 8, size)
    return pl.pallas_call(
        analysis_kernel,
        grid=(owned // tiles,),
        in_specs=[packed, packed, packed, block(tiles, size, width)],
        out_specs=block(tiles, size, width),
        out_shape=jax.ShapeDtypeStruct(states.shape, F32),
        scratch_shapes=[pltpu.VMEM((tiles, size, size), F32)] * 2,
        cost_estimate=pl.CostEstimate(
            flops=owned * 27 * 12 * size**3, bytes_accessed=states.size * 8, transcendentals=0
        ),
        compiler_params=pltpu.CompilerParams(vmem_limit_bytes=56 * 2**20),
    )(own, west, east, states)


def shards(chunks, members, obs_value, obs_precision, obs_index, obs_count):
    owned = members.shape[1] // lax.axis_size("member")
    parts = chunks if owned % chunks == 0 else 1
    first_band = lax.axis_index("member") * owned
    per = owned // parts
    count = lax.axis_size("member")
    rows, tiles, width = members.shape

    def own_rows(tables):
        return lax.dynamic_slice_in_dim(tables, first_band, owned, 0)

    filled = own_rows(obs_count)
    slot_ids = jnp.arange(obs_value.shape[1], dtype=jnp.int32)
    accuracy = jnp.where(slot_ids[None] < filled[:, None], own_rows(obs_precision), 0.0)
    places, observed = own_rows(obs_index), own_rows(obs_value)

    turned = members.reshape(rows, count, parts, per, width).transpose(2, 1, 3, 0, 4)
    columns = lax.axis_size("region")
    forward = [(i, (i + 1) % columns) for i in range(columns)]
    backward = [(b, a) for a, b in forward]
    gathered, packed = [], []
    for i in range(parts):
        got = lax.all_to_all(turned[i], "member", split_axis=0, concat_axis=0, tiled=False)
        got = got.transpose(1, 0, 2, 3).reshape(per, count * rows, width)
        span = slice(i * per, (i + 1) * per)
        own = grams(got, places[span], observed[span], accuracy[span])
        gathered.append(got)
        packed.append(
            (own, lax.ppermute(own, "region", forward), lax.ppermute(own, "region", backward))
        )
    results = []
    for i in range(parts):
        result = analyses(*packed[i], gathered[i])
        result = result.reshape(per, count, rows, width).transpose(1, 0, 2, 3)
        results.append(lax.all_to_all(result, "member", split_axis=0, concat_axis=0, tiled=False))
    return jnp.stack(results, axis=1).reshape(tiles, rows, width).transpose(1, 0, 2)


def solution(mesh):
    in_specs = (
        P("member", "region", None),
        P("region", None),
        P("region", None),
        P("region", None),
        P("region"),
    )
    out_specs = P("member", "region", None)
    return jax.shard_map(
        functools.partial(shards, 1),
        mesh=mesh,
        in_specs=in_specs,
        out_specs=out_specs,
        check_vma=False,
    )
```

profile of v0, /device:TPU:0, one launch (start us, length us, event | category | flops | bytes accessed | tf_op | source)
XLA Modules:
  0.0 213.0 jit_solution(7297065657048837653)
XLA Ops:
  0.0 0.0 copy-start
  0.0 6.7 %copy.8 = f32[64,16,1024]{2,0,1:T(8,128)} copy(f32[64,16,1024]{2,1,0:T(8,128)} %param.5) | data formatting | bytes 8388608 | tf_op args[0]
  6.7 5.0 %all-to-all-start = ((f32[4,4,64,1024]{3,2,1,0:T(8,128)}), f32[4,4,64,1024]{3,2,1,0:T(8,128)}, u32[]{:S(2)}, u32[]{:S(2)}) async-start(f32[4,4,64,1024]{3,2,1,0:T(8,128)} %bitcast.15), calls=%async_computation | async-start | bytes 8388608 | tf_op jit(solution)/shard_map/all_to_all | solution.py:210
  11.6 0.0 copy-done.3
  11.7 0.1 dynamic_slice.14
  11.7 0.0 copy-done
  11.7 0.6 broadcast_in_dim.15.index_ref
  12.4 0.8 dynamic-slice_select_fusion
  13.2 0.6 broadcast_in_dim.18.precision_ref
  13.8 0.6 broadcast_in_dim.16.value_ref
  14.4 46.1 %all-to-all-done = f32[4,4,64,1024]{3,2,1,0:T(8,128)} async-done(((f32[4,4,64,1024]{3,2,1,0:T(8,128)}), f32[4,4,64,1024]{3,2,1,0:T(8,128)}, u32[]{:S(2)}, u32[]{:S(2)}) %all-to-all-start) | async-done | bytes 4194336 | tf_op jit(solution)/shard_map/all_to_all | solution.py:210
  60.5 4.8 %copy.9 = f32[4,4,64,1024]{3,2,1,0:T(8,128)} copy(f32[4,4,64,1024]{3,2,0,1:T(8,128)} %bitcast.3) | data formatting | bytes 8388608 | tf_op jit(solution)/shard_map/transpose | solution.py:211
  65.3 8.1 %shard_map.55.own_ref = f32[4,136,256]{2,1,0:T(8,128)} custom-call(f32[4,256,1024]{2,1,0:T(8,128)} %bitcast.18, s32[4,1,1024]{2,1,0:T(1,128)} %broadcast_in_dim.15.index_ref, f32[4,1,1024]{2,1,0:T(1,128)} %broadcast_in_dim.16.value_ref, f32[4,1,1024]{2,1,0:T(1,128)} %broadcast_in_dim.18.precision_ref), custom_call_target="tpu_custom_call" | custom-call | flops 3221225472 | bytes 4194304 | tf_op jit(solution)/shard_map/pallas_call | solution.py:158
  73.4 5.3 %collective-permute-start.1 = (f32[4,136,256]{2,1,0:T(8,128)}, f32[4,136,256]{2,1,0:T(8,128)S(1)}, u32[]{:S(2)}, u32[]{:S(2)}) collective-permute-start(f32[4,136,256]{2,1,0:T(8,128)} %shard_map.55.own_ref), channel_id=1, source_target_pairs={{4,0},{8,4},{12,8},{16,12},{20,16},{24,20},{28,24},{0,28},{5,1},{9... | collective-permute-start | bytes 1671176 | tf_op jit(solution)/shard_map/ppermute | solution.py:216
  78.7 0.0 collective-permute-start
  78.7 21.4 %collective-permute-done.1.east_ref = f32[4,136,256]{2,1,0:T(8,128)S(1)} collective-permute-done((f32[4,136,256]{2,1,0:T(8,128)}, f32[4,136,256]{2,1,0:T(8,128)S(1)}, u32[]{:S(2)}, u32[]{:S(2)}) %collective-permute-start.1) | collective-permute-done | bytes 557088 | tf_op jit(solution)/shard_map/ppermute | solution.py:216
  100.1 0.0 copy-start.1
  100.2 0.3 collective-permute-done.west_ref
  100.4 0.6 copy-done.1
  101.0 0.8 copy-done.2
  101.8 53.5 %shard_map.56 = f32[4,256,1024]{2,1,0:T(8,128)} custom-call(f32[4,136,256]{2,1,0:T(8,128)} %shard_map.55.own_ref, f32[4,136,256]{2,1,0:T(8,128)} %copy-done.2, f32[4,136,256]{2,1,0:T(8,128)} %copy-done.1, f32[4,256,1024]{2,1,0:T(8,128)} %bitcast.19), custom_call_target="tpu_custom_call" | custom-call | flops 21743271936 | bytes 8388608 | tf_op jit(solution)/shard_map/pallas_call | solution.py:174
  155.4 2.5 %copy.15 = f32[4,4,64,1024]{3,2,0,1:T(8,128)S(1)} copy(f32[4,4,64,1024]{3,2,1,0:T(8,128)} %bitcast.20) | data formatting | bytes 8388608 | tf_op jit(solution)/shard_map/reshape | solution.py:221
  157.9 50.7 %all_to_all.10 = f32[4,4,64,1024]{3,2,1,0:T(8,128)S(1)} all-to-all(f32[4,4,64,1024]{3,2,1,0:T(8,128)S(1)} %bitcast.16), channel_id=1, replica_groups=mesh['region'=8,'member'=4] {'member'}, dimensions={0} | all-to-all | bytes 8388608 | tf_op jit(solution)/shard_map/all_to_all | solution.py:222
  208.6 4.4 %copy.14 = f32[16,64,1024]{2,0,1:T(8,128)} copy(f32[16,64,1024]{2,1,0:T(8,128)S(1)} %bitcast.17) | data formatting | bytes 8388608 | tf_op jit(solution)/shard_map/reshape;stack | solution.py:223
  (3 shorter events, 0.0 us)
Async XLA Ops:
  0.0 11.7 %copy-start = (s32[16,1024]{1,0:T(8,128)S(1)}, s32[16,1024]{1,0:T(8,128)}, u32[]{:S(2)}) copy-start(s32[16,1024]{1,0:T(8,128)} %param.8) | copy-start | bytes 196612
  6.7 5.0 %copy-start.3 = (s32[16]{0:T(128)S(1)}, s32[16]{0:T(128)}, u32[]{:S(2)}) copy-start(s32[16]{0:T(128)} %param.9) | copy-start | bytes 196
  6.7 53.9 %all-to-all-start = ((f32[4,4,64,1024]{3,2,1,0:T(8,128)}), f32[4,4,64,1024]{3,2,1,0:T(8,128)}, u32[]{:S(2)}, u32[]{:S(2)}) async-start(f32[4,4,64,1024]{3,2,1,0:T(8,128)} %bitcast.15), calls=%async_computation | async-start | bytes 8388608 | tf_op jit(solution)/shard_map/all_to_all | solution.py:210
  73.4 26.7 %collective-permute-start.1 = (f32[4,136,256]{2,1,0:T(8,128)}, f32[4,136,256]{2,1,0:T(8,128)S(1)}, u32[]{:S(2)}, u32[]{:S(2)}) collective-permute-start(f32[4,136,256]{2,1,0:T(8,128)} %shard_map.55.own_ref), channel_id=1, source_target_pairs={{4,0},{8,4},{12,8},{16,12},{20,16},{24,20},{28,24},{0,28},{5,1},{9... | collective-permute-start | bytes 1671176 | tf_op jit(solution)/shard_map/ppermute | solution.py:216
  78.7 21.7 %collective-permute-start = (f32[4,136,256]{2,1,0:T(8,128)}, f32[4,136,256]{2,1,0:T(8,128)S(1)}, u32[]{:S(2)}, u32[]{:S(2)}) collective-permute-start(f32[4,136,256]{2,1,0:T(8,128)} %shard_map.55.own_ref), channel_id=1, source_target_pairs={{0,4},{4,8},{8,12},{12,16},{16,20},{20,24},{24,28},{28,0},{1,5},{5... | collective-permute-start | bytes 1671176 | tf_op jit(solution)/shard_map/ppermute | solution.py:216
  100.1 0.8 copy-start.1
  101.0 0.8 copy-start.2
where the time goes:
time: 213 us
  waiting for transfers between devices  67.8 us (32%)
  Pallas kernels  61.6 us (29%)
  blocking collectives  50.7 us (24%)
  local copies, waits for them, and re-layouts  21.7 us (10%)
  starting transfers between devices  10.3 us (5%)
    pallas_call x1, Pallas kernels, analyses(): pl.pallas_call(analysis_kernel, grid=(owned // tiles,), in_specs=[packed,...  53.5 us
    all_to_all x1, blocking collectives, shards(): lax.all_to_all(result, 'member', split_axis=0, concat_axis=0, tiled=False)  50.7 us
    all_to_all x1, waiting for transfers between devices, shards(): lax.all_to_all(turned[i], 'member', split_axis=0, concat_axis=0, tiled=Fa...  46.1 us
    ppermute x1, waiting for transfers between devices, shards(): lax.ppermute(own, 'region', backward)  21.4 us
    pallas_call x1, Pallas kernels, grams(): pl.pallas_call(gram_kernel, grid=(owned,), in_specs=[block(1, size, width...  8.07 us
    unnamed x9, local copies, waits for them, and re-layouts  8.06 us
    ppermute x1, starting transfers between devices, shards(): lax.ppermute(own, 'region', backward)  5.3 us
    all_to_all x1, starting transfers between devices, shards(): lax.all_to_all(turned[i], 'member', split_axis=0, concat_axis=0, tiled=Fa...  4.97 us
  transfers between devices with their start and end apart: 3, of which 3 were waited for; matrix products, arithmetic and copies ran while one was open for 1% of the time, Pallas kernels for 0%

commit v1 on v0

v1 whole, which is shorter than its diff:
```python
import functools
import math

import jax
import jax.numpy as jnp
from jax import lax
from jax.experimental import pallas as pl
from jax.experimental.pallas import tpu as pltpu
from jax.sharding import PartitionSpec as P

ITERS = 12
LANES = 128
MESH = pl.DeviceIdType.MESH
F32 = jnp.float32
BF16 = jnp.bfloat16


def split3(x):
    a = x.astype(BF16)
    rest = x - a.astype(F32)
    b = rest.astype(BF16)
    return a, b, (rest - b.astype(F32)).astype(BF16)


def dot(a, b):
    return jnp.dot(a, b, preferred_element_type=F32)


def dot_nt(a, b):
    return lax.dot_general(a, b, (((1,), (1,)), ((), ())), preferred_element_type=F32)


def product(a, b):
    a1, a2, a3 = a
    b1, b2, b3 = b
    left = jnp.concatenate([a1, a3, a2, a1, a2, a1], axis=1)
    right = jnp.concatenate([b3, b1, b2, b2, b1, b1], axis=0)
    return dot(left, right)


def gram(states, places, exact, observed):
    size, width = states.shape
    half = size // 2
    groups = width // LANES
    slots = places.shape[1]

    high = lax.shift_right_logical(places, 7)
    low = lax.bitwise_and(places, LANES - 1)
    rows = lax.broadcasted_iota(jnp.int32, (groups, slots), 0) == high
    both = jnp.concatenate(
        [jnp.where(rows, exact, 0.0), jnp.where(rows, exact * observed, 0.0)], axis=0
    )
    one_hot = jnp.where(
        lax.broadcasted_iota(jnp.int32, (LANES, slots), 0) == low, 1.0, 0.0
    ).astype(BF16)
    e1, e2, e3 = split3(both)
    sums = dot_nt(e3, one_hot) + dot_nt(e2, one_hot) + dot_nt(e1, one_hot)
    c = jnp.concatenate([sums[i : i + 1] for i in range(groups)], axis=1)
    d = jnp.concatenate([sums[groups + i : groups + i + 1] for i in range(groups)], axis=1)

    average = jnp.sum(states, axis=0, keepdims=True) / size
    deviation = states - average
    s1, s2, s3 = split3(deviation * jnp.sqrt(c))
    cross = dot_nt(s1, s3) + dot_nt(s1, s2)
    own = (dot_nt(s2, s2) + (cross + cross.T)) + dot_nt(s1, s1)

    pulled = deviation * (d - c * average)
    folded = pulled[:, :LANES]
    for i in range(1, groups):
        folded = folded + pulled[:, i * LANES : (i + 1) * LANES]
    right = jnp.sum(folded.T, axis=0, keepdims=True)

    row = lax.broadcasted_iota(jnp.int32, (half, half), 0)
    col = lax.broadcasted_iota(jnp.int32, (half, half), 1)
    first, last = own[:half, :half], own[half:, half:]
    diagonal = jnp.sum(jnp.where(row == col, last, 0.0), axis=0, keepdims=True)
    square = jnp.concatenate([own[:half, half:], jnp.where(row <= col, first, last)], axis=1)
    tail = jnp.concatenate([right, jnp.concatenate([diagonal, diagonal], axis=1)], axis=0)
    return square, jnp.concatenate([tail, jnp.zeros((6, size), F32)], axis=0)


def unpack(packed, size):
    half = size // 2
    row = lax.broadcasted_iota(jnp.int32, (half, half), 0)
    col = lax.broadcasted_iota(jnp.int32, (half, half), 1)
    upper, mixed = packed[:half, :half], packed[:half, half:]
    right = packed[half : half + 1]
    diagonal = packed[half + 1 : half + 2, :half]
    turned = mixed.T
    first = jnp.where(row <= col, mixed, turned)
    last = jnp.where(row > col, mixed, turned)
    last = jnp.where(row == col, diagonal, last)
    full = jnp.concatenate(
        [
            jnp.concatenate([first, upper], axis=1),
            jnp.concatenate([upper.T, last], axis=1),
        ],
        axis=0,
    )
    return full, right


def identity_of(size):
    row = lax.broadcasted_iota(jnp.int32, (size, size), 0)
    col = lax.broadcasted_iota(jnp.int32, (size, size), 1)
    return jnp.where(row == col, 1.0, 0.0).astype(F32)


def growth(u, z, size):
    identity = identity_of(size)
    x = split3(u if z is None else product(z, u))
    plain = u if z is None else x[0].astype(F32) + x[1].astype(F32) + x[2].astype(F32)
    squared = product(x, x)
    inner = (1 / 16) * squared - (9 / 16) * plain
    outer = product(split3(squared), split3(inner))
    return (36 / 16) * identity - (39 / 16) * plain + (27 / 16) * squared + outer


def kernel(
    count, columns,
    x_hbm, value_ref, precision_ref, index_ref, filled_ref, out_ref,
    x_ref, send_ref, got_ref, own_ref, west_ref, east_ref, result_ref,
    u_ref, z_ref, right_ref, scale_ref,
    x_sem, in_send, in_recv, gram_send, gram_recv, out_send, out_recv, out_local,
):
    me, column = lax.axis_index("member"), lax.axis_index("region")
    owned, size, width = got_ref.shape
    tiles = owned * count
    rows = size // count
    slots = index_ref.shape[1]
    half = size // 2

    def peer(k):
        return lax.rem(me + k, count)

    x_copy = pltpu.make_async_copy(x_hbm, x_ref, x_sem)
    x_copy.start()
    beside = (lax.rem(column + 1, columns), lax.rem(column + columns - 1, columns))
    barrier = pltpu.get_barrier_semaphore()
    for k in range(1, count):
        pl.semaphore_signal(barrier, inc=1, device_id={"member": peer(k)}, device_id_type=MESH)
    for b in beside:
        pl.semaphore_signal(barrier, inc=1, device_id={"region": b}, device_id_type=MESH)
    pl.semaphore_wait(barrier, count + 1)

    def in_copy(j, k):
        return pltpu.make_async_remote_copy(
            src_ref=send_ref.at[j, peer(k)],
            dst_ref=got_ref.at[j, pl.ds(pl.multiple_of(me * rows, rows), rows)],
            send_sem=in_send.at[j, k - 1],
            recv_sem=in_recv.at[j, k - 1],
            device_id={"member": peer(k)},
            device_id_type=MESH,
        )

    def out_copy(j, k):
        return pltpu.make_async_remote_copy(
            src_ref=result_ref.at[j, pl.ds(pl.multiple_of(peer(k) * rows, rows), rows)],
            dst_ref=out_ref.at[j * count + me],
            send_sem=out_send.at[j, k - 1],
            recv_sem=out_recv.at[j, k - 1],
            device_id={"member": peer(k)},
            device_id_type=MESH,
        )

    def gram_copy(j, side):
        return pltpu.make_async_remote_copy(
            src_ref=own_ref.at[j],
            dst_ref=(west_ref, east_ref)[side].at[j],
            send_sem=gram_send.at[j, side],
            recv_sem=gram_recv.at[j, side],
            device_id={"region": beside[side]},
            device_id_type=MESH,
        )

    x_copy.wait()

    def scatter(j, carry):
        for q in range(count):
            send_ref[j, q] = x_ref[:, j * count + q, :]
        for k in range(1, count):
            in_copy(j, k).start()
        got_ref[j, pl.ds(pl.multiple_of(me * rows, rows), rows)] = send_ref[j, me]
        return carry

    lax.fori_loop(0, owned, scatter, 0)

    def make_gram(j):
        for k in range(1, count):
            in_copy(j, k).wait_recv()
        t = j * count + me
        slot = lax.broadcasted_iota(jnp.int32, (1, slots), 1)
        exact = jnp.where(slot < filled_ref[t], precision_ref[pl.ds(t, 1), :], 0.0)
        square, tail = gram(
            got_ref[j], index_ref[pl.ds(t, 1), :], exact, value_ref[pl.ds(t, 1), :]
        )
        own_ref[j, :half] = square
        own_ref[j, half:] = tail
        for side in range(2):
            gram_copy(j, side).start()

    def two_steps(_, carry):
        u, z = split3(u_ref[...]), split3(z_ref[...])
        g = split3(growth(u, z, size))
        u_ref[...] = product(u, g)
        z_ref[...] = product(g, z)
        return carry

    make_gram(0)
    loops = ITERS // 2 - 2

    def analyse(j, carry):
        for side in range(2):
            gram_copy(j, side).wait_recv()
        full, right = unpack(own_ref[j] + 0.5 * (west_ref[j] + east_ref[j]), size)
        system = (size - 1.0) * identity_of(size) + full
        total = jnp.sum(jnp.sum(system * system, axis=0, keepdims=True), axis=1, keepdims=True)
        scale = jnp.sqrt(total + 1e-6)
        right_ref[...] = right
        scale_ref[...] = jnp.broadcast_to(scale, (1, LANES))
        u = system / scale
        g = growth(u, None, size)
        z_ref[...] = g
        u_ref[...] = product(split3(u), split3(g))
        lax.fori_loop(0, loops // 2, two_steps, 0)

        @pl.when(j + 1 < owned)
        def _():
            make_gram(j + 1)

        lax.fori_loop(loops // 2, loops, two_steps, 0)
        u, z = split3(u_ref[...]), split3(z_ref[...])
        inverse = product(split3(growth(u, z, size)), z) / jnp.sqrt(scale_ref[:, :1])
        pulled = jnp.sum(inverse * right_ref[...], axis=1, keepdims=True)
        shift = jnp.sum(inverse * pulled, axis=0, keepdims=True)
        weights = math.sqrt(size - 1.0) * inverse + shift
        states = got_ref[j]
        average = jnp.sum(states, axis=0, keepdims=True) / size
        w1, w2, _ = split3(weights)
        d1, d2, _ = split3(states - average)
        left = jnp.concatenate([w2, w1, w1], axis=1)
        right = jnp.concatenate([d1, d2, d1], axis=0)
        result_ref[j] = average + dot(left, right)
        for k in range(1, count):
            out_copy(j, k).start()
        pltpu.make_async_copy(
            result_ref.at[j, pl.ds(pl.multiple_of(me * rows, rows), rows)],
            out_ref.at[j * count + me],
            out_local.at[j],
        ).start()
        return carry

    lax.fori_loop(0, owned, analyse, 0)

    def finish(j, carry):
        for k in range(1, count):
            in_copy(j, k).wait_send()
            out_copy(j, k).wait()
        for side in range(2):
            gram_copy(j, side).wait_send()
        pltpu.make_async_copy(
            result_ref.at[j, pl.ds(pl.multiple_of(me * rows, rows), rows)],
            out_ref.at[j * count + me],
            out_local.at[j],
        ).wait()
        return carry

    lax.fori_loop(0, owned, finish, 0)


def shards(members, obs_value, obs_precision, obs_index, obs_count):
    count, columns = lax.axis_size("member"), lax.axis_size("region")
    rows, tiles, width = members.shape
    owned = tiles // count
    size = count * rows
    packed = pltpu.VMEM((owned, size // 2 + 8, size), F32)
    whole = pl.BlockSpec(memory_space=pltpu.VMEM)
    anywhere = pl.BlockSpec(memory_space=pl.ANY)
    dma = pltpu.SemaphoreType.DMA
    out = pl.pallas_call(
        functools.partial(kernel, count, columns),
        in_specs=[anywhere, whole, whole, whole, pl.BlockSpec(memory_space=pltpu.SMEM)],
        out_specs=anywhere,
        out_shape=jax.ShapeDtypeStruct((tiles, rows, width), F32),
        scratch_shapes=[
            pltpu.VMEM((rows, tiles, width), F32),
            pltpu.VMEM((owned, count, rows, width), F32),
            pltpu.VMEM((owned, size, width), F32),
            packed, packed, packed,
            pltpu.VMEM((owned, size, width), F32),
            pltpu.VMEM((size, size), F32),
            pltpu.VMEM((size, size), F32),
            pltpu.VMEM((1, size), F32),
            pltpu.VMEM((1, LANES), F32),
            dma,
            dma((owned, count - 1)),
            dma((owned, count - 1)),
            dma((owned, 2)),
            dma((owned, 2)),
            dma((owned, count - 1)),
            dma((owned, count - 1)),
            dma((owned,)),
        ],
        compiler_params=pltpu.CompilerParams(
            collective_id=0, has_side_effects=True, vmem_limit_bytes=60 * 2**20
        ),
    )(members, obs_value, obs_precision, obs_index, obs_count)
    return out.transpose(1, 0, 2)


def solution(mesh):
    in_specs = (
        P("member", "region", None),
        P("region", None),
        P("region", None),
        P("region", None),
        P("region"),
    )
    return jax.shard_map(
        shards,
        mesh=mesh,
        in_specs=in_specs,
        out_specs=P("member", "region", None),
        check_vma=False,
    )
```

time: 213 us -> 106 us (0.50)
  waiting for transfers between devices: 67.8 us -> 0 us
  blocking collectives: 50.7 us -> 0 us
  Pallas kernels: 61.6 us -> 97.7 us
  local copies, waits for them, and re-layouts: 21.7 us -> 6.63 us
  starting transfers between devices: 10.3 us -> 0 us
    all_to_all x1 -> x0, blocking collectives: 50.7 us -> none  [shards(): lax.all_to_all(result, 'member', split_axis=0, concat_axis=0, tiled=False)]
    all_to_all x1 -> x0, waiting for transfers between devices: 46.1 us -> none  [shards(): lax.all_to_all(turned[i], 'member', split_axis=0, concat_axis=0, tiled=Fa...]
    pallas_call x2 -> x1, Pallas kernels: 61.6 us -> 97.7 us  [shards(): pl.pallas_call(functools.partial(kernel, count, columns), in_specs=[anywh...]
    ppermute x2 -> x0, waiting for transfers between devices: 21.7 us -> none  [the longest x1 21.4 us: shards(): lax.ppermute(own, 'region', backward)]
    unnamed x9 -> x0, local copies, waits for them, and re-layouts: 8.06 us -> none
    ppermute x2 -> x0, starting transfers between devices: 5.3 us -> none  [the longest x1 5.3 us: shards(): lax.ppermute(own, 'region', backward)]
    all_to_all x1 -> x0, starting transfers between devices: 4.97 us -> none  [shards(): lax.all_to_all(turned[i], 'member', split_axis=0, concat_axis=0, tiled=Fa...]
    another operation x1 -> x0, local copies, waits for them, and re-layouts: 4.44 us -> none  [shards(): jnp.stack(results, axis=1).reshape(tiles, rows, width).transpose(1, 0, 2)]
  transfers between devices with their start and end apart: 3 -> 0, of which waited for: 3 -> 0; matrix products, arithmetic and copies ran while one was open for 1% -> 0% of each run, Pallas kernels for 0% -> 0%
where the time goes in v1:
time: 106 us; the launch traced here: 104 us
  Pallas kernels  97.7 us (92%)
  local copies, waits for them, and re-layouts  6.63 us (6%)
    pallas_call x1, Pallas kernels, shards(): pl.pallas_call(functools.partial(kernel, count, columns), in_specs=[anywh...  97.7 us
    transpose x1, local copies, waits for them, and re-layouts, shards(): return out.transpose(1, 0, 2)  6.63 us

profile of v1, /device:TPU:0, one launch (start us, length us, event | category | flops | bytes accessed | tf_op | source)
XLA Modules:
  0.0 104.3 jit_solution(17767011504335505899)
XLA Ops:
  0.0 97.7 %shard_map.55 = f32[16,64,1024]{2,1,0:T(8,128)} custom-call(f32[64,16,1024]{2,1,0:T(8,128)} %x_hbm.1, f32[16,1024]{1,0:T(8,128)} %value_ref.1, f32[16,1024]{1,0:T(8,128)} %precision_ref.1, s32[16,1024]{1,0:T(8,128)} %index_ref.1, s32[16]{0:T(128)} %filled_ref.1), custom_call_target="tpu_custom_call" | custom-call | tf_op jit(solution)/shard_map/pallas_call | solution.py:280
  97.7 6.6 %copy.6 = f32[64,16,1024]{2,1,0:T(8,128)} copy(f32[64,16,1024]{2,0,1:T(8,128)} %bitcast.1) | data formatting | bytes 8388608 | tf_op jit(solution)/shard_map/transpose | solution.py:308

commit v2 on v1

--- a/solution.py
+++ b/solution.py
@@ -118,10 +118,10 @@
 
 def kernel(
     count, columns,
-    x_hbm, value_ref, precision_ref, index_ref, filled_ref, out_ref,
-    x_ref, send_ref, got_ref, own_ref, west_ref, east_ref, result_ref,
+    x_hbm, value_hbm, precision_hbm, index_hbm, filled_hbm, out_ref,
+    value_ref, precision_ref, index_ref, filled_ref, got_ref, own_ref, west_ref, east_ref, result_ref,
     u_ref, z_ref, right_ref, scale_ref,
-    x_sem, in_send, in_recv, gram_send, gram_recv, out_send, out_recv, out_local,
+    x_sem, table_sem, go_sem, open_sem, in_send, in_recv, gram_send, gram_recv, out_send, out_recv,
 ):
     me, column = lax.axis_index("member"), lax.axis_index("region")
     owned, size, width = got_ref.shape
@@ -133,19 +133,70 @@
     def peer(k):
         return lax.rem(me + k, count)
 
-    x_copy = pltpu.make_async_copy(x_hbm, x_ref, x_sem)
-    x_copy.start()
+    def own_copy(j):
+        return pltpu.make_async_copy(
+            x_hbm.at[:, j * count + me, :],
+            got_ref.at[j, pl.ds(pl.multiple_of(me * rows, rows), rows)],
+            x_sem.at[j],
+        )
+
+    tables = (
+        (value_hbm, value_ref),
+        (precision_hbm, precision_ref),
+        (index_hbm, index_ref),
+        (filled_hbm, filled_ref),
+    )
+    table_copies = [
+        pltpu.make_async_copy(a, b, table_sem.at[i]) for i, (a, b) in enumerate(tables)
+    ]
+    for copy in table_copies:
+        copy.start()
+
     beside = (lax.rem(column + 1, columns), lax.rem(column + columns - 1, columns))
     barrier = pltpu.get_barrier_semaphore()
+    staggered = count % 2 == 0 and columns % 2 == 0
+    free = lax.rem(column + me, 2) == 0
+    partner = me + 1 - 2 * lax.rem(me, 2)
+
+    def greet(semaphore):
+        for b in beside:
+            pl.semaphore_signal(semaphore, inc=1, device_id={"region": b}, device_id_type=MESH)
+
     for k in range(1, count):
         pl.semaphore_signal(barrier, inc=1, device_id={"member": peer(k)}, device_id_type=MESH)
-    for b in beside:
-        pl.semaphore_signal(barrier, inc=1, device_id={"region": b}, device_id_type=MESH)
-    pl.semaphore_wait(barrier, count + 1)
+    if staggered:
+
+        @pl.when(free)
+        def _():
+            pl.semaphore_wait(barrier, count - 1)
+            pl.semaphore_signal(
+                go_sem, inc=1, device_id={"member": partner}, device_id_type=MESH
+            )
+            greet(barrier)
+
+        @pl.when(jnp.logical_not(free))
+        def _():
+            pl.semaphore_wait(go_sem, 1)
+
+    else:
+        greet(barrier)
+        pl.semaphore_wait(barrier, count + 1)
+
+    def meet_region():
+        if staggered:
+
+            @pl.when(free)
+            def _():
+                pl.semaphore_wait(open_sem, 2)
+
+            @pl.when(jnp.logical_not(free))
+            def _():
+                pl.semaphore_wait(barrier, count + 1)
+                greet(open_sem)
 
     def in_copy(j, k):
         return pltpu.make_async_remote_copy(
-            src_ref=send_ref.at[j, peer(k)],
+            src_ref=x_hbm.at[:, j * count + peer(k), :],
             dst_ref=got_ref.at[j, pl.ds(pl.multiple_of(me * rows, rows), rows)],
             send_sem=in_send.at[j, k - 1],
             recv_sem=in_recv.at[j, k - 1],
@@ -156,7 +207,7 @@
     def out_copy(j, k):
         return pltpu.make_async_remote_copy(
             src_ref=result_ref.at[j, pl.ds(pl.multiple_of(peer(k) * rows, rows), rows)],
-            dst_ref=out_ref.at[j * count + me],
+            dst_ref=out_ref.at[:, j * count + me, :],
             send_sem=out_send.at[j, k - 1],
             recv_sem=out_recv.at[j, k - 1],
             device_id={"member": peer(k)},
@@ -173,19 +224,17 @@
             device_id_type=MESH,
         )
 
-    x_copy.wait()
-
-    def scatter(j, carry):
-        for q in range(count):
-            send_ref[j, q] = x_ref[:, j * count + q, :]
+    for j in range(owned):
         for k in range(1, count):
             in_copy(j, k).start()
-        got_ref[j, pl.ds(pl.multiple_of(me * rows, rows), rows)] = send_ref[j, me]
-        return carry
-
-    lax.fori_loop(0, owned, scatter, 0)
+    for j in range(owned):
+        own_copy(j).start()
+    for copy in table_copies:
+        copy.wait()
+    meet_region()
 
     def make_gram(j):
+        own_copy(j).wait()
         for k in range(1, count):
             in_copy(j, k).wait_recv()
         t = j * count + me
@@ -243,11 +292,7 @@
         result_ref[j] = average + dot(left, right)
         for k in range(1, count):
             out_copy(j, k).start()
-        pltpu.make_async_copy(
-            result_ref.at[j, pl.ds(pl.multiple_of(me * rows, rows), rows)],
-            out_ref.at[j * count + me],
-            out_local.at[j],
-        ).start()
+        out_ref[:, j * count + me, :] = result_ref[j, pl.ds(pl.multiple_of(me * rows, rows), rows)]
         return carry
 
     lax.fori_loop(0, owned, analyse, 0)
@@ -258,11 +303,6 @@
             out_copy(j, k).wait()
         for side in range(2):
             gram_copy(j, side).wait_send()
-        pltpu.make_async_copy(
-            result_ref.at[j, pl.ds(pl.multiple_of(me * rows, rows), rows)],
-            out_ref.at[j * count + me],
-            out_local.at[j],
-        ).wait()
         return carry
 
     lax.fori_loop(0, owned, finish, 0)
@@ -275,16 +315,18 @@
     size = count * rows
     packed = pltpu.VMEM((owned, size // 2 + 8, size), F32)
     whole = pl.BlockSpec(memory_space=pltpu.VMEM)
-    anywhere = pl.BlockSpec(memory_space=pl.ANY)
+    table = obs_value.shape
     dma = pltpu.SemaphoreType.DMA
     out = pl.pallas_call(
         functools.partial(kernel, count, columns),
-        in_specs=[anywhere, whole, whole, whole, pl.BlockSpec(memory_space=pltpu.SMEM)],
-        out_specs=anywhere,
-        out_shape=jax.ShapeDtypeStruct((tiles, rows, width), F32),
+        in_specs=[pl.BlockSpec(memory_space=pltpu.HBM)] * 5,
+        out_specs=whole,
+        out_shape=jax.ShapeDtypeStruct((rows, tiles, width), F32),
         scratch_shapes=[
-            pltpu.VMEM((rows, tiles, width), F32),
-            pltpu.VMEM((owned, count, rows, width), F32),
+            pltpu.VMEM(table, F32),
+            pltpu.VMEM(table, F32),
+            pltpu.VMEM(table, jnp.int32),
+            pltpu.SMEM(obs_count.shape, jnp.int32),
             pltpu.VMEM((owned, size, width), F32),
             packed, packed, packed,
             pltpu.VMEM((owned, size, width), F32),
@@ -292,20 +334,25 @@
             pltpu.VMEM((size, size), F32),
             pltpu.VMEM((1, size), F32),
             pltpu.VMEM((1, LANES), F32),
-            dma,
+            dma((owned,)),
+            dma((4,)),
+            pltpu.SemaphoreType.REGULAR,
+            pltpu.SemaphoreType.REGULAR,
             dma((owned, count - 1)),
             dma((owned, count - 1)),
             dma((owned, 2)),
             dma((owned, 2)),
             dma((owned, count - 1)),
             dma((owned, count - 1)),
-            dma((owned,)),
         ],
         compiler_params=pltpu.CompilerParams(
-            collective_id=0, has_side_effects=True, vmem_limit_bytes=60 * 2**20
+            collective_id=0, has_side_effects=True, vmem_limit_bytes=44 * 2**20
         ),
-    )(members, obs_value, obs_precision, obs_index, obs_count)
-    return out.transpose(1, 0, 2)
+    )(*(
+        pltpu.with_memory_space_constraint(a, pltpu.HBM)
+        for a in (members, obs_value, obs_precision, obs_index, obs_count)
+    ))
+    return out
 
 
 def solution(mesh):

time: 106 us -> 96.8 us (0.913); the launches traced: 104 us -> 96.7 us
  local copies, waits for them, and re-layouts: 6.63 us -> 2.02 us
  Pallas kernels: 97.7 us -> 94.7 us
    transpose x1 -> x0, local copies, waits for them, and re-layouts: 6.63 us -> none  [shards(): return out.transpose(1, 0, 2)]
    pallas_call x1, Pallas kernels: 97.7 us -> 94.7 us  [shards(): pl.pallas_call(functools.partial(kernel, count, columns), in_specs=[pl.Bl...]
    unnamed x0 -> x1, local copies, waits for them, and re-layouts: none -> 2.02 us
where the time goes in v2:
time: 96.8 us; the launch traced here: 96.7 us
  Pallas kernels  94.7 us (98%)
  local copies, waits for them, and re-layouts  2.02 us (2%)
    pallas_call x1, Pallas kernels, shards(): pl.pallas_call(functools.partial(kernel, count, columns), in_specs=[pl.Bl...  94.7 us
    unnamed x1, local copies, waits for them, and re-layouts  2.02 us

profile of v2, /device:TPU:0, one launch (start us, length us, event | category | flops | bytes accessed | tf_op | source)
XLA Modules:
  0.0 96.7 jit_solution(11507738977427490800)
XLA Ops:
  0.0 94.7 %shard_map.55 = f32[64,16,1024]{2,1,0:T(8,128)S(1)} custom-call(f32[64,16,1024]{2,1,0:T(8,128)} %x_hbm.1, f32[16,1024]{1,0:T(8,128)} %value_hbm.1, f32[16,1024]{1,0:T(8,128)} %precision_hbm.1, s32[16,1024]{1,0:T(8,128)} %index_hbm.1, s32[16]{0:T(128)} %filled_hbm.1), custom_call_target="tpu_custom_call" | custom-call | tf_op jit(solution)/shard_map/pallas_call | solution.py:320
  94.7 2.0 %copy.7 = f32[64,16,1024]{2,1,0:T(8,128)} copy(f32[64,16,1024]{2,1,0:T(8,128)S(1)} %shard_map.55) | data formatting | bytes 8388608

commit v3 on v2

--- a/solution.py
+++ b/solution.py
@@ -149,50 +149,51 @@
     table_copies = [
         pltpu.make_async_copy(a, b, table_sem.at[i]) for i, (a, b) in enumerate(tables)
     ]
-    for copy in table_copies:
-        copy.start()
 
     beside = (lax.rem(column + 1, columns), lax.rem(column + columns - 1, columns))
     barrier = pltpu.get_barrier_semaphore()
-    staggered = count % 2 == 0 and columns % 2 == 0
-    free = lax.rem(column + me, 2) == 0
+    paired = count % 2 == 0
+    first = lax.rem(me, 2) == 0
     partner = me + 1 - 2 * lax.rem(me, 2)
 
-    def greet(semaphore):
+    def greet():
         for b in beside:
-            pl.semaphore_signal(semaphore, inc=1, device_id={"region": b}, device_id_type=MESH)
+            pl.semaphore_signal(barrier, inc=1, device_id={"region": b}, device_id_type=MESH)
+
+    def tell(semaphore):
+        pl.semaphore_signal(
+            semaphore, inc=1, device_id={"member": partner}, device_id_type=MESH
+        )
 
     for k in range(1, count):
         pl.semaphore_signal(barrier, inc=1, device_id={"member": peer(k)}, device_id_type=MESH)
-    if staggered:
-
-        @pl.when(free)
+    if paired:
+
+        @pl.when(first)
         def _():
             pl.semaphore_wait(barrier, count - 1)
-            pl.semaphore_signal(
-                go_sem, inc=1, device_id={"member": partner}, device_id_type=MESH
-            )
-            greet(barrier)
-
-        @pl.when(jnp.logical_not(free))
+            tell(go_sem)
+
+        @pl.when(jnp.logical_not(first))
         def _():
             pl.semaphore_wait(go_sem, 1)
 
     else:
-        greet(barrier)
+        greet()
         pl.semaphore_wait(barrier, count + 1)
 
     def meet_region():
-        if staggered:
-
-            @pl.when(free)
+        if paired:
+
+            @pl.when(first)
             def _():
-                pl.semaphore_wait(open_sem, 2)
-
-            @pl.when(jnp.logical_not(free))
+                pl.semaphore_wait(open_sem, 1)
+
+            @pl.when(jnp.logical_not(first))
             def _():
+                greet()
                 pl.semaphore_wait(barrier, count + 1)
-                greet(open_sem)
+                tell(open_sem)
 
     def in_copy(j, k):
         return pltpu.make_async_remote_copy(
@@ -229,6 +230,8 @@
             in_copy(j, k).start()
     for j in range(owned):
         own_copy(j).start()
+    for copy in table_copies:
+        copy.start()
     for copy in table_copies:
         copy.wait()
     meet_region()
@@ -290,9 +293,9 @@
         left = jnp.concatenate([w2, w1, w1], axis=1)
         right = jnp.concatenate([d1, d2, d1], axis=0)
         result_ref[j] = average + dot(left, right)
+        out_ref[:, j * count + me, :] = result_ref[j, pl.ds(pl.multiple_of(me * rows, rows), rows)]
         for k in range(1, count):
             out_copy(j, k).start()
-        out_ref[:, j * count + me, :] = result_ref[j, pl.ds(pl.multiple_of(me * rows, rows), rows)]
         return carry
 
     lax.fori_loop(0, owned, analyse, 0)

time: 96.8 us -> 96.8 us (level)
  no operation moved by 1% of the time
where the time goes in v3:
time: 96.8 us; the launch traced here: 96.7 us
  Pallas kernels  94.7 us (98%)
  local copies, waits for them, and re-layouts  2.02 us (2%)
    pallas_call x1, Pallas kernels, shards(): pl.pallas_call(functools.partial(kernel, count, columns), in_specs=[pl.Bl...  94.7 us
    unnamed x1, local copies, waits for them, and re-layouts  2.02 us

profile of v3, /device:TPU:0, one launch (start us, length us, event | category | flops | bytes accessed | tf_op | source)
XLA Modules:
  0.0 96.7 jit_solution(725744528830507593)
XLA Ops:
  0.0 94.7 %shard_map.55 = f32[64,16,1024]{2,1,0:T(8,128)S(1)} custom-call(f32[64,16,1024]{2,1,0:T(8,128)} %x_hbm.1, f32[16,1024]{1,0:T(8,128)} %value_hbm.1, f32[16,1024]{1,0:T(8,128)} %precision_hbm.1, s32[16,1024]{1,0:T(8,128)} %index_hbm.1, s32[16]{0:T(128)} %filled_hbm.1), custom_call_target="tpu_custom_call" | custom-call | tf_op jit(solution)/shard_map/pallas_call | solution.py:323
  94.7 2.0 %copy.7 = f32[64,16,1024]{2,1,0:T(8,128)} copy(f32[64,16,1024]{2,1,0:T(8,128)S(1)} %shard_map.55) | data formatting | bytes 8388608

commit v4 on v3

--- a/solution.py
+++ b/solution.py
@@ -225,8 +225,9 @@
             device_id_type=MESH,
         )
 
+    farthest_first = sorted(range(1, count), key=lambda k: abs(2 * k - count))
     for j in range(owned):
-        for k in range(1, count):
+        for k in farthest_first:
             in_copy(j, k).start()
     for j in range(owned):
         own_copy(j).start()
@@ -309,6 +310,26 @@
         return carry
 
     lax.fori_loop(0, owned, finish, 0)
+
+
+def flush_kernel(held_ref, out_hbm, sem):
+    copy = pltpu.make_async_copy(held_ref, out_hbm, sem)
+    copy.start()
+    copy.wait()
+
+
+def flush(held):
+    return pl.pallas_call(
+        flush_kernel,
+        in_specs=[pl.BlockSpec(memory_space=pltpu.VMEM)],
+        out_specs=pl.BlockSpec(memory_space=pltpu.HBM),
+        out_shape=jax.ShapeDtypeStruct(held.shape, held.dtype),
+        scratch_shapes=[pltpu.SemaphoreType.DMA],
+        cost_estimate=pl.CostEstimate(
+            flops=0, bytes_accessed=held.size * 4, transcendentals=0
+        ),
+        compiler_params=pltpu.CompilerParams(vmem_limit_bytes=16 * 2**20),
+    )(held)
 
 
 def shards(members, obs_value, obs_precision, obs_index, obs_count):
@@ -355,7 +376,7 @@
         pltpu.with_memory_space_constraint(a, pltpu.HBM)
         for a in (members, obs_value, obs_precision, obs_index, obs_count)
     ))
-    return out
+    return flush(out)
 
 
 def solution(mesh):

time: 96.8 us -> 98 us (1.012); the launches traced: 96.7 us -> 96.7 us
  local copies, waits for them, and re-layouts: 2.02 us -> 0 us
  Pallas kernels: 94.7 us -> 96.7 us
    pallas_call x0 -> x1, Pallas kernels: none -> 2.02 us  [flush(): pl.pallas_call(flush_kernel, in_specs=[pl.BlockSpec(memory_space=pltpu.VM...]
    unnamed x1 -> x0, local copies, waits for them, and re-layouts: 2.02 us -> none
where the time goes in v4:
time: 98 us; the launch traced here: 96.7 us
  Pallas kernels  96.7 us (99%)
    pallas_call x1, Pallas kernels, shards(): pl.pallas_call(functools.partial(kernel, count, columns), in_specs=[pl.Bl...  94.7 us
    pallas_call x1, Pallas kernels, flush(): pl.pallas_call(flush_kernel, in_specs=[pl.BlockSpec(memory_space=pltpu.VM...  2.02 us

profile of v4, /device:TPU:0, one launch (start us, length us, event | category | flops | bytes accessed | tf_op | source)
XLA Modules:
  0.0 96.7 jit_solution(484148779730867555)
XLA Ops:
  0.0 94.7 %shard_map.55.held_ref = f32[64,16,1024]{2,1,0:T(8,128)S(1)} custom-call(f32[64,16,1024]{2,1,0:T(8,128)} %x_hbm.1, f32[16,1024]{1,0:T(8,128)} %value_hbm.1, f32[16,1024]{1,0:T(8,128)} %precision_hbm.1, s32[16,1024]{1,0:T(8,128)} %index_hbm.1, s32[16]{0:T(128)} %filled_hbm.1), custom_call_target="tpu_custom_call" | custom-call | tf_op jit(solution)/shard_map/pallas_call | solution.py:344
  94.7 2.0 %shard_map.56 = f32[64,16,1024]{2,1,0:T(8,128)} custom-call(f32[64,16,1024]{2,1,0:T(8,128)S(1)} %shard_map.55.held_ref), custom_call_target="tpu_custom_call" | custom-call | bytes 4194304 | tf_op jit(solution)/shard_map/pallas_call | solution.py:322

commit v5 on v4

--- a/solution.py
+++ b/solution.py
@@ -225,9 +225,8 @@
             device_id_type=MESH,
         )
 
-    farthest_first = sorted(range(1, count), key=lambda k: abs(2 * k - count))
     for j in range(owned):
-        for k in farthest_first:
+        for k in range(1, count):
             in_copy(j, k).start()
     for j in range(owned):
         own_copy(j).start()

time: 98 us -> 96.8 us (0.988); the launches traced: 96.7 us -> 96.7 us
  no operation moved by 1% of the time
where the time goes in v5:
time: 96.8 us; the launch traced here: 96.7 us
  Pallas kernels  96.7 us (100%)
    pallas_call x1, Pallas kernels, shards(): pl.pallas_call(functools.partial(kernel, count, columns), in_specs=[pl.Bl...  94.7 us
    pallas_call x1, Pallas kernels, flush(): pl.pallas_call(flush_kernel, in_specs=[pl.BlockSpec(memory_space=pltpu.VM...  2.02 us

profile of v5, /device:TPU:0, one launch (start us, length us, event | category | flops | bytes accessed | tf_op | source)
XLA Modules:
  0.0 96.7 jit_solution(8522247541902511168)
XLA Ops:
  0.0 94.7 %shard_map.55.held_ref = f32[64,16,1024]{2,1,0:T(8,128)S(1)} custom-call(f32[64,16,1024]{2,1,0:T(8,128)} %x_hbm.1, f32[16,1024]{1,0:T(8,128)} %value_hbm.1, f32[16,1024]{1,0:T(8,128)} %precision_hbm.1, s32[16,1024]{1,0:T(8,128)} %index_hbm.1, s32[16]{0:T(128)} %filled_hbm.1), custom_call_target="tpu_custom_call" | custom-call | tf_op jit(solution)/shard_map/pallas_call | solution.py:343
  94.7 2.0 %shard_map.56 = f32[64,16,1024]{2,1,0:T(8,128)} custom-call(f32[64,16,1024]{2,1,0:T(8,128)S(1)} %shard_map.55.held_ref), custom_call_target="tpu_custom_call" | custom-call | bytes 4194304 | tf_op jit(solution)/shard_map/pallas_call | solution.py:321
